TPU v7x, 256 devices: a whole 4x4x8 slice. The times are simulated.
256 devices in a mesh: rep: 2 (over core), dp: 128 (over x, y, z).
Axes of the slice: x: 4, y: 4, z: 8, core: 2. Of those that a mesh axis runs over, the one named last changes fastest.
Arguments:
- x: bfloat16 [256, 2048, 896], P(('rep', 'dp')), parts along dimension 0
- dy: bfloat16 [256, 2048, 896], P(('rep', 'dp')), parts along dimension 0
- w_gate: bfloat16 [2, 896, 2560], replicated
- w_up: bfloat16 [2, 896, 2560], replicated
- w_down: bfloat16 [2, 2560, 896], replicated
- m_w_gate: float32 [2, 896, 2560], replicated
- m_w_up: float32 [2, 896, 2560], replicated
- m_w_down: float32 [2, 2560, 896], replicated
- v_w_gate: float32 [2, 896, 2560], replicated
- v_w_up: float32 [2, 896, 2560], replicated
- v_w_down: float32 [2, 2560, 896], replicated
Outputs:
- output 1: bfloat16 [4, 896, 2560], P('rep'), parts along dimension 0
- output 2: bfloat16 [4, 896, 2560], P('rep'), parts along dimension 0
- output 3: bfloat16 [4, 2560, 896], P('rep'), parts along dimension 0
- output 4: float32 [4, 896, 2560], P('rep'), parts along dimension 0
- output 5: float32 [4, 896, 2560], P('rep'), parts along dimension 0
- output 6: float32 [4, 2560, 896], P('rep'), parts along dimension 0
- output 7: float32 [4, 896, 2560], P('rep'), parts along dimension 0
- output 8: float32 [4, 896, 2560], P('rep'), parts along dimension 0
- output 9: float32 [4, 2560, 896], P('rep'), parts along dimension 0
There are 2 independent parts. A program takes and returns all parts, laid end to end along the dimension named above; an argument that names none is the same for every part.
All inputs are finite; a program needn't handle non-finite values.
Results may differ from a plain program's by a relative error of at most 0.022.
Values are sent between devices in bfloat16 or wider.
A program may use at most 768 MiB of HBM per device.

v0:
```python
import jax
import jax.numpy as jnp
from jax import lax
from jax.sharding import PartitionSpec as P

NAMES = ("w_gate", "w_up", "w_down")


def matmul(a, w):
    return jnp.dot(a, w, preferred_element_type=jnp.float32).astype(jnp.bfloat16)


def normed(h):
    wide = h.astype(jnp.float32)
    scale = lax.rsqrt(jnp.mean(wide**2, -1, keepdims=True) + 1e-6)
    return (wide * scale).astype(jnp.bfloat16)


def layer(h, w):
    a = normed(h)
    gate = jnp.dot(a, w["w_gate"], preferred_element_type=jnp.float32)
    up = jnp.dot(a, w["w_up"], preferred_element_type=jnp.float32)
    return h + matmul((jax.nn.silu(gate) * up).astype(jnp.bfloat16), w["w_down"])


def adamw(w, m, v, g):
    m = 0.9 * m + 0.1 * g
    v = 0.95 * v + 0.05 * g * g
    step = m * lax.rsqrt(v + 1e-8) + 0.1 * w
    return (w - 0.02 * step).astype(jnp.bfloat16), m, v


def clipped(gradients, sum_of_squares, count):
    factor = jnp.minimum(1.0, 0.5 * lax.rsqrt(sum_of_squares / count + 1e-30))
    return [g * factor for g in gradients]


def solution(mesh):
    def step(x, dy, *arrays):
        weights, m, v = (arrays[i : i + 3] for i in (0, 3, 6))
        layers = weights[0].shape[0]
        h, kept = x[0], []
        for number in range(layers):
            kept.append(h)
            h = layer(h, {name: w[number] for name, w in zip(NAMES, weights, strict=True)})
        by_h, summed = dy[0], [None] * layers
        for number in reversed(range(layers)):
            _, back = jax.vjp(lambda w, h: layer(h, w), {name: w[number] for name, w in zip(NAMES, weights, strict=True)}, kept[number])
            by_w, by_h = back(by_h)
            summed[number] = [lax.psum(by_w[name], "dp") for name in NAMES]
        gradients = [jnp.stack([summed[number][i] for number in range(layers)]).astype(jnp.float32) for i in range(3)]
        gradients = clipped(gradients, sum(jnp.sum(g * g) for g in gradients), sum(g.size for g in gradients))
        new = [adamw(w.astype(jnp.float32), m, v, g) for w, m, v, g in zip(weights, m, v, gradients, strict=True)]
        return tuple(one[which] for which in range(3) for one in new)

    return jax.shard_map(
        step,
        mesh=mesh,
        in_specs=(P(("rep", "dp"), None, None),) * 2 + (P(None, None, None),) * 9,
        out_specs=(P("rep", None, None),) * 9,
        check_vma=False,
    )
```

profile of v0, /device:TPU:2, one launch (start us, length us, event | category | flops | bytes accessed | tf_op | source)
XLA Modules:
  0.0 909.2 jit_solution(4378197565642507855)
XLA Ops:
  7.2 0.0 all-reduce.3.cloned.1.call-start
  7.2 6.1 copy.20
  13.3 2.8 fusion.36
  16.1 0.0 copy-start.8
  16.1 0.0 slice-start.2
  16.1 6.2 copy.21
  22.3 0.0 slice-start.3
  22.4 0.0 slice-start.4
  22.4 0.0 copy-start.3
  22.4 16.6 %convolution_convert_fusion.1 = bf16[2048,2560]{1,0:T(8,128)(2,1)} fusion(bf16[2,2560,896]{2,1,0:T(8,128)(2,1)} %param.15, bf16[1,2048,896]{2,1,0:T(8,128)(2,1)} %param.12), kind=kOutput, calls=%fused_computation.63 | convolution fusion | flops 9400483840 | bytes 18743296 | tf_op jit(solution)/shard_map/transpose(jvp())/dot_general | solution.py:10
  39.0 0.0 slice-done.2
  39.0 0.0 slice-done.3
  39.0 0.0 slice-done.4
  39.0 0.0 copy-done.3
  39.0 14.1 %fusion.70 = f32[2048,2560]{1,0:T(8,128)} fusion(bf16[2,896,2560]{2,1,0:T(8,128)(2,1)S(1)} %bitcast.77, bf16[1,2048,896]{2,1,0:T(8,128)(2,1)S(1)} %copy-done.3, f32[2048]{0:T(1024)S(1)} %add_rsqrt_fusion), kind=kOutput, calls=%fused_computation.105 | convolution fusion | flops 9400745984 | bytes 29237248 | tf_op jit(solution)/shard_map/dot_general | solution.py:21
  53.1 0.0 copy-done.8
  53.1 0.0 copy-start.1
  53.1 26.3 %multiply_convert_fusion.1 = (bf16[2048,2560]{1,0:T(8,128)(2,1)}, f32[2048,2560]{1,0:T(8,128)}) fusion(f32[2048,2560]{1,0:T(8,128)} %fusion.70, bf16[2,896,2560]{2,1,0:T(8,128)(2,1)} %param.14, bf16[1,2048,896]{2,1,0:T(8,128)(2,1)} %param.11, f32[2048]{0:T(1024)S(1)} %add_rsqrt_fusion), kind=kOutput, calls=%fused_computation.35 | convolution fusion | flops 9432203264 | bytes 60694528 | tf_op jit(solution)/shard_map/dot_general | solution.py:22
  79.4 0.0 copy-done.1
  79.5 14.8 %fusion.40 = (f32[2048]{0:T(1024)S(1)}, bf16[2048,896]{0,1:T(8,128)(2,1)S(1)}) fusion(bf16[2048,2560]{1,0:T(8,128)(2,1)} %get-tuple-element.24, bf16[2,2560,896]{2,1,0:T(8,128)(2,1)} %param.15, bf16[1,2048,896]{1,2,0:T(8,128)(2,1)S(1)} %copy-done.1), kind=kOutput, calls=%fused_computation.76 | convolution fusion | flops 9404413952 | bytes 22421504 | tf_op jit(solution)/shard_map/dot_general | solution.py:10
  94.2 0.0 copy-start.6
  94.2 0.0 copy-start.4
  94.2 0.6 copy-done.6
  94.8 1.2 copy-done.4
  96.1 17.0 %fusion.57 = f32[2048,2560]{1,0:T(8,128)} fusion(bf16[2,896,2560]{2,1,0:T(8,128)(2,1)} %param.14, bf16[2048,896]{0,1:T(8,128)(2,1)S(1)} %get-tuple-element.27, f32[2048]{0:T(1024)S(1)} %fusion.98), kind=kOutput, calls=%fused_computation.92 | convolution fusion | flops 9400745984 | bytes 29237248 | tf_op jit(solution)/shard_map/jvp()/dot_general | solution.py:22
  113.1 31.9 %fusion.5 = (bf16[2048,2560]{1,0:T(8,128)(2,1)}, f32[2048,2560]{1,0:T(8,128)}) fusion(f32[2048,2560]{1,0:T(8,128)} %fusion.57, bf16[2048,2560]{1,0:T(8,128)(2,1)} %convolution_convert_fusion.1, bf16[2,896,2560]{2,1,0:T(8,128)(2,1)} %param.13, bf16[2048,896]{0,1:T(8,128)(2,1)} %copy-done.4, f32[2048]{0:T(1024)S(1)} %fusion.98), kind=kOutput, calls=%fused_computation.26 | convolution fusion | flops 9463660544 | bytes 71180288 | tf_op jit(solution)/shard_map/jvp()/dot_general | solution.py:21
  145.1 18.1 %fusion.33 = bf16[2048,896]{0,1:T(8,128)(2,1)} fusion(bf16[2048,2560]{1,0:T(8,128)(2,1)} %convolution_convert_fusion.1, bf16[2,896,2560]{2,1,0:T(8,128)(2,1)} %param.14, f32[2048,2560]{1,0:T(8,128)} %get-tuple-element.29), kind=kOutput, calls=%fused_computation.57 | convolution fusion | flops 9426698240 | bytes 39714816 | tf_op jit(solution)/shard_map/transpose(jvp())/dot_general | solution.py:22
  163.2 18.6 %fusion.51 = bf16[1,896,2560]{2,1,0:T(8,128)(2,1)} fusion(bf16[2048,2560]{1,0:T(8,128)(2,1)} %convolution_convert_fusion.1, bf16[2048,896]{0,1:T(8,128)(2,1)} %copy-done.4, f32[2048]{0:T(1024)S(1)} %fusion.98, f32[2048,2560]{1,0:T(8,128)} %get-tuple-element.29), kind=kOutput, calls=%fused_computation.88 | convolution fusion | flops 9434497024 | bytes 39723008 | tf_op jit(solution)/shard_map/transpose(jvp())/dot_general | solution.py:22
  181.8 21.3 %fusion.49 = bf16[1,2560,896]{2,1,0:T(8,128)(2,1)} fusion(f32[2048,2560]{1,0:T(8,128)} %fusion.57, bf16[1,2048,896]{2,1,0:T(8,128)(2,1)} %param.12, f32[2048,2560]{1,0:T(8,128)} %get-tuple-element.29), kind=kOutput, calls=%fused_computation.86 | convolution fusion | flops 9428992000 | bytes 50200576 | tf_op jit(solution)/shard_map/transpose(jvp())/dot_general | solution.py:10
  203.1 0.0 slice-start.5
  203.1 0.0 slice-start.6
  203.1 15.4 %fusion.52 = bf16[1,896,2560]{2,1,0:T(8,128)(2,1)} fusion(bf16[2048,2560]{1,0:T(8,128)(2,1)} %get-tuple-element.28, bf16[2048,896]{0,1:T(8,128)(2,1)} %copy-done.4, f32[2048]{0:T(1024)S(1)} %fusion.98), kind=kOutput, calls=%fused_computation.89 | convolution fusion | flops 9400745984 | bytes 18751488 | tf_op jit(solution)/shard_map/transpose(jvp())/dot_general | solution.py:21
  218.6 0.0 copy-start.7
  218.6 0.0 copy-start.2
  218.6 0.0 slice-start.7
  218.6 17.0 %fusion.42 = (f32[2048]{0:T(1024)S(1)}, bf16[2048,896]{0,1:T(8,128)(2,1)}) fusion(bf16[2048,896]{0,1:T(8,128)(2,1)} %copy-done.4, bf16[2048,896]{0,1:T(8,128)(2,1)} %fusion.33, bf16[2048,2560]{1,0:T(8,128)(2,1)} %get-tuple-element.28, bf16[2,896,2560]{2,1,0:T(8,128)(2,1)} %param.13), kind=kOutput, calls=%fused_computation.78 | convolution fusion | flops 9404413952 | bytes 26091520 | tf_op jit(solution)/shard_map/transpose(jvp())/dot_general | solution.py:21
  235.6 0.0 copy-done.7
  235.6 0.0 copy-done.2
  235.6 7.6 fusion.82
  243.2 0.0 slice-done.5
  243.2 0.0 slice-done.6
  243.3 0.0 slice-done.7
  243.3 0.0 copy-start.5
  243.3 15.7 %convolution_convert_fusion = bf16[2048,2560]{1,0:T(8,128)(2,1)} fusion(bf16[2048,896]{0,1:T(8,128)(2,1)} %fusion.82, bf16[2,2560,896]{2,1,0:T(8,128)(2,1)S(1)} %bitcast.79), kind=kOutput, calls=%fused_computation.62 | convolution fusion | flops 9400483840 | bytes 18743296 | tf_op jit(solution)/shard_map/transpose(jvp())/dot_general | solution.py:10
  258.9 0.0 copy-done.5
  258.9 0.0 copy-start.9
  258.9 15.4 %fusion.53 = bf16[1,2560,896]{2,1,0:T(8,128)(2,1)} fusion(bf16[2048,2560]{1,0:T(8,128)(2,1)} %get-tuple-element.24, bf16[2048,896]{0,1:T(8,128)(2,1)S(1)} %copy-done.5), kind=kOutput, calls=%fused_computation.90 | convolution fusion | flops 9397534720 | bytes 18743296 | tf_op jit(solution)/shard_map/transpose(jvp())/dot_general | solution.py:10
  274.4 0.0 copy-done.9
  274.4 18.7 %fusion.50 = bf16[1,896,2560]{2,1,0:T(8,128)(2,1)} fusion(bf16[2048,2560]{1,0:T(8,128)(2,1)} %convolution_convert_fusion, f32[2048,2560]{1,0:T(8,128)} %fusion.70, bf16[1,2048,896]{1,2,0:T(8,128)(2,1)} %copy.20, f32[2048]{0:T(1024)S(1)} %copy-done.9), kind=kOutput, calls=%fused_computation.87 | convolution fusion | flops 9434497024 | bytes 39723008 | tf_op jit(solution)/shard_map/transpose(jvp())/dot_general | solution.py:22
  293.0 24.3 %fusion.54 = bf16[1,896,2560]{2,1,0:T(8,128)(2,1)} fusion(f32[2048,2560]{1,0:T(8,128)} %fusion.70, f32[2048,2560]{1,0:T(8,128)} %get-tuple-element.25, bf16[2048,2560]{1,0:T(8,128)(2,1)} %convolution_convert_fusion, bf16[1,2048,896]{1,2,0:T(8,128)(2,1)} %copy.20, f32[2048]{0:T(1024)S(1)} %copy-done.9), kind=kOutput, calls=%fused_computation.91 | convolution fusion | flops 9460711424 | bytes 60694528 | tf_op jit(solution)/shard_map/transpose(jvp())/dot_general | solution.py:21
  317.3 0.0 all-reduce.3.cloned.1.call-update
  317.4 455.7 %all-reduce.3.cloned.1.call-done = (bf16[1,896,2560]{2,1,0:T(8,128)(2,1)}, bf16[1,896,2560]{2,1,0:T(8,128)(2,1)}, bf16[1,896,2560]{2,1,0:T(8,128)(2,1)}, bf16[1,...) async-done(((bf16[1,896,2560]{2,1,0:T(8,128)(2,1)}, bf16[1,896,2560]{2,1,0:T(8,128)(2,1)}, bf16[1,896,2560]{2,1,0:T(8,128)(2,1)}, ...) | async-done | bytes 27525136 | tf_op jit(solution)/shard_map/psum | solution.py:50
  773.1 0.0 slice-start
  773.1 0.0 copy-start
  773.1 0.0 slice-start.1
  773.1 9.2 %fusion.20 = f32[]{:T(128)} fusion(bf16[1,896,2560]{2,1,0:T(8,128)(2,1)} %get-tuple-element.9, bf16[1,896,2560]{2,1,0:T(8,128)(2,1)} %get-tuple-element.10), kind=kLoop, calls=%fused_computation.44 | loop fusion | flops 18350080 | bytes 9175044 | tf_op jit(solution)/shard_map/reduce_sum | solution.py:52
  782.2 0.0 slice-done
  782.2 0.0 copy-done
  782.2 0.0 slice-done.1
  782.2 5.3 fusion.21
  788.9 9.0 fusion.22
  798.6 36.0 %fusion.28 = (bf16[2,2560,896]{2,1,0:T(8,128)(2,1)}, f32[2,2560,896]{2,1,0:T(8,128)}, f32[2,2560,896]{2,1,0:T(8,128)}) fusion(bf16[2,2560,896]{2,1,0:T(8,128)(2,1)} %param.15, f32[]{:T(128)S(6)} %min_shard_map.3, bf16[1,2560,896]{2,1,0:T(8,128)(2,1)} %get-tuple-element.13, bf16[1,2560,896]{2,1,0:T(8,128)(2,1)} %get-tuple-element.14, ...), kind=kLoop, calls=%fused_computation.52 | loop fusion | flops 91750400 | bytes 100925440 | tf_op jit(solution)/shard_map/convert_element_type | solution.py:30
  834.5 67.4 %fusion.19 = (bf16[2,896,2560]{2,1,0:T(8,128)(2,1)}, f32[2,896,2560]{2,1,0:T(8,128)}, f32[2,896,2560]{2,1,0:T(8,128)}, bf16[2,896,2560]{2,1,0:T(8,128)(2,1)}, f3...) fusion(bf16[2,896,2560]{2,1,0:T(8,128)(2,1)} %param.13, f32[]{:T(128)S(6)} %min_shard_map.3, ...), kind=kLoop, calls=%fused_computation.43 | loop fusion | flops 183500800 | bytes 201850880 | tf_op jit(solution)/shard_map/convert_element_type | solution.py:30
  (6 shorter events, 0.0 us)
Async XLA Ops:
  7.2 765.9 %all-reduce.3.cloned.1.call-start = ((), (), s32[]{:S(2)}) async-start(), calls=%async_computation | async-start | bytes 55050240 | tf_op jit(solution)/shard_map/psum | solution.py:50
  16.1 37.0 %copy-start.8 = (f32[2048]{0:T(1024)}, f32[2048]{0:T(1024)S(1)}, u32[]{:S(2)}) copy-start(f32[2048]{0:T(1024)S(1)} %add_rsqrt_fusion) | copy-start | bytes 24580
  16.1 22.9 %slice-start.2 = ((s8[9175040]{0:T(1024)(128)(4,1)}), s8[786432]{0:T(1024)(128)(4,1)S(1)}, s32[]{:S(2)}) async-start(s8[9175040]{0:T(1024)(128)(4,1)} %bitcast.76), calls=%async_computation.3 | async-start | bytes 1572864
  22.3 16.6 %slice-start.3 = ((s8[9175040]{0:T(1024)(128)(4,1)}), s8[4194304]{0:T(1024)(128)(4,1)S(1)}, s32[]{:S(2)}) async-start(s8[9175040]{0:T(1024)(128)(4,1)} %bitcast.76), calls=%async_computation.4 | async-start | bytes 8388608
  22.4 16.6 %slice-start.4 = ((s8[9175040]{0:T(1024)(128)(4,1)}), s8[4194304]{0:T(1024)(128)(4,1)S(1)}, s32[]{:S(2)}) async-start(s8[9175040]{0:T(1024)(128)(4,1)} %bitcast.76), calls=%async_computation.5 | async-start | bytes 8388608
  22.4 16.6 %copy-start.3 = (bf16[1,2048,896]{2,1,0:T(8,128)(2,1)S(1)}, bf16[1,2048,896]{2,1,0:T(8,128)(2,1)}, u32[]{:S(2)}) copy-start(bf16[1,2048,896]{2,1,0:T(8,128)(2,1)} %param.11) | copy-start | bytes 11010052
  53.1 26.3 %copy-start.1 = (bf16[1,2048,896]{1,2,0:T(8,128)(2,1)S(1)}, bf16[1,2048,896]{1,2,0:T(8,128)(2,1)}, u32[]{:S(2)}) copy-start(bf16[1,2048,896]{1,2,0:T(8,128)(2,1)} %copy.20) | copy-start | bytes 11010052
  94.2 0.6 copy-start.6
  94.2 1.8 copy-start.4
  203.1 40.1 %slice-start.5 = ((s8[9175040]{0:T(1024)(128)(4,1)}), s8[4194304]{0:T(1024)(128)(4,1)S(1)}, s32[]{:S(2)}) async-start(s8[9175040]{0:T(1024)(128)(4,1)} %bitcast.78), calls=%async_computation.6 | async-start | bytes 8388608
  203.1 40.1 %slice-start.6 = ((s8[9175040]{0:T(1024)(128)(4,1)}), s8[4194304]{0:T(1024)(128)(4,1)S(1)}, s32[]{:S(2)}) async-start(s8[9175040]{0:T(1024)(128)(4,1)} %bitcast.78), calls=%async_computation.7 | async-start | bytes 8388608
  218.6 17.0 %copy-start.7 = (f32[2048]{0:T(1024)S(1)}, f32[2048]{0:T(1024)}, u32[]{:S(2)}) copy-start(f32[2048]{0:T(1024)} %copy-done.6) | copy-start | bytes 24580
  218.6 17.0 %copy-start.2 = (bf16[1,2048,896]{1,2,0:T(8,128)(2,1)S(1)}, bf16[1,2048,896]{1,2,0:T(8,128)(2,1)}, u32[]{:S(2)}) copy-start(bf16[1,2048,896]{1,2,0:T(8,128)(2,1)} %copy.21) | copy-start | bytes 11010052
  218.6 24.7 %slice-start.7 = ((s8[9175040]{0:T(1024)(128)(4,1)}), s8[786432]{0:T(1024)(128)(4,1)S(1)}, s32[]{:S(2)}) async-start(s8[9175040]{0:T(1024)(128)(4,1)} %bitcast.78), calls=%async_computation.8 | async-start | bytes 1572864
  243.3 15.7 %copy-start.5 = (bf16[2048,896]{0,1:T(8,128)(2,1)S(1)}, bf16[2048,896]{0,1:T(8,128)(2,1)}, u32[]{:S(2)}) copy-start(bf16[2048,896]{0,1:T(8,128)(2,1)} %fusion.82) | copy-start | bytes 11010052
  258.9 15.4 %copy-start.9 = (f32[2048]{0:T(1024)S(1)}, f32[2048]{0:T(1024)}, u32[]{:S(2)}) copy-start(f32[2048]{0:T(1024)} %copy-done.8) | copy-start | bytes 24580
  773.1 9.2 %slice-start = ((s8[4587520]{0:T(1024)(128)(4,1)}), s8[4194304]{0:T(1024)(128)(4,1)S(1)}, s32[]{:S(2)}) async-start(s8[4587520]{0:T(1024)(128)(4,1)} %bitcast.74), calls=%async_computation.1 | async-start | bytes 8388608
  773.1 9.2 %copy-start = (bf16[1,896,2560]{2,1,0:T(8,128)(2,1)S(1)}, bf16[1,896,2560]{2,1,0:T(8,128)(2,1)}, u32[]{:S(2)}) copy-start(bf16[1,896,2560]{2,1,0:T(8,128)(2,1)} %get-tuple-element.12) | copy-start | bytes 13762564
  773.1 9.2 %slice-start.1 = ((s8[4587520]{0:T(1024)(128)(4,1)}), s8[393216]{0:T(1024)(128)(4,1)S(1)}, s32[]{:S(2)}) async-start(s8[4587520]{0:T(1024)(128)(4,1)} %bitcast.74), calls=%async_computation.2 | async-start | bytes 786432
Sparse Core Ops, SparseCore 0:
  317.5 455.5 all-reduce.2
where the time goes:
time: 917 us; the launch traced here: 909 us
  waiting for transfers between devices  456 us (50%)
  matrix products  285 us (31%)
  other arithmetic  137 us (15%)
  between operations  16.6 us (2%)
  local copies, waits for them, and re-layouts  14.2 us (2%)
    psum x1, waiting for transfers between devices, step(): summed[number] = [lax.psum(by_w[name], 'dp') for name in NAMES]  456 us
    convert_element_type x2, other arithmetic, adamw(): return ((w - 0.02 * step).astype(jnp.bfloat16), m, v)  103 us
    dot_general x5, matrix products, layer(): gate = jnp.dot(a, w['w_gate'], preferred_element_type=jnp.float32)  103 us
    dot_general x5, matrix products, layer(): up = jnp.dot(a, w['w_up'], preferred_element_type=jnp.float32)  98.8 us
    dot_general x5, matrix products, matmul(): jnp.dot(a, w, preferred_element_type=jnp.float32).astype(jnp.bfloat16)  83.7 us
    reduce_sum x3, other arithmetic, step(): jnp.sum(g * g)  23.5 us
  transfers between devices with their start and end apart: 1, of which 1 were waited for; matrix products, arithmetic and copies ran while one was open for 0% of the time, Pallas kernels for 0%

commit v1 on v0

v1 whole, which is shorter than its diff:
```python
import functools

import jax
import jax.numpy as jnp
from jax import lax
from jax.experimental import pallas as pl
from jax.experimental.pallas import tpu as pltpu
from jax.sharding import PartitionSpec as P

F32, BF16 = jnp.float32, jnp.bfloat16
S, D, FF = 2048, 896, 2560
MESH = pl.DeviceIdType.MESH
ANY = pl.BlockSpec(memory_space=pl.ANY)
TILE = (16, 128)
NT = 1152
SLAB = 384
SIZE = {"x": 4, "y": 4, "z": 8}
STRIDE = {"x": 32, "y": 8, "z": 1}
COLORS = (("x", "y", "z"), ("y", "x", "z"), ("z", "x", "y"))
RECV = 381
NN = (((1,), (0,)), ((), ()))
NT_ = (((1,), (1,)), ((), ()))
TN = (((0,), (0,)), ((), ()))


def dot(a, b, dims=NN):
    return lax.dot_general(a, b, dims, preferred_element_type=F32)


def norm_of(h):
    wide = h.astype(F32)
    return wide, lax.rsqrt(jnp.mean(wide * wide, -1, keepdims=True) + 1e-6)


def activations_kernel(CH, x_ref, dy_ref, wg_hbm, wu_hbm, wd_hbm, a0_ref, z0_ref, dg0_ref, du0_ref, a1_ref, z1_ref, dg1_ref, du1_ref, dh_ref, wg, wu, wd, gate0, up0, sem):
    first = pl.program_id(0) == 0
    n = FF // CH
    copies = [[pltpu.make_async_copy(hbm.at[layer], vmem.at[layer], sem.at[layer, k]) for k, (hbm, vmem) in enumerate(((wg_hbm, wg), (wu_hbm, wu), (wd_hbm, wd)))] for layer in range(2)]

    @pl.when(first)
    def _():
        for layer in range(2):
            for copy in copies[layer]:
                copy.start()
        copies[0][0].wait()
        copies[0][1].wait()

    x = x_ref[...]
    dy = dy_ref[...]
    wide, scale = norm_of(x)
    a = (wide * scale).astype(BF16)
    a0_ref[...] = a
    for j in range(n):
        at = pl.ds(j * CH, CH)
        gate, up = dot(a, wg[0, :, at]), dot(a, wu[0, :, at])
        gate0[:, at] = gate
        up0[:, at] = up
        z0_ref[:, at] = (gate * (0.5 + 0.5 * jnp.tanh(0.5 * gate)) * up).astype(BF16)

    @pl.when(first)
    def _():
        copies[0][2].wait()

    h = x + dot(z0_ref[...], wd[0]).astype(BF16)
    wide, scale = norm_of(h)
    a = (wide * scale).astype(BF16)
    a1_ref[...] = a

    @pl.when(first)
    def _():
        for copy in copies[1]:
            copy.wait()

    def back(gate, up, dz, dg_ref, du_ref, at):
        dz = dz.astype(BF16).astype(F32)
        sig = 0.5 + 0.5 * jnp.tanh(0.5 * gate)
        silu = gate * sig
        du_ref[:, at] = (dz * silu).astype(BF16)
        dg_ref[:, at] = (dz * up * (sig + silu * (1.0 - sig))).astype(BF16)
        return silu

    for j in range(n):
        at = pl.ds(j * CH, CH)
        gate, up, dz = dot(a, wg[1, :, at]), dot(a, wu[1, :, at]), dot(dy, wd[1, at, :], NT_)
        z1_ref[:, at] = (back(gate, up, dz, dg1_ref, du1_ref, at) * up).astype(BF16)
    da = (dot(dg1_ref[...], wg[1], NT_).astype(BF16) + dot(du1_ref[...], wu[1], NT_).astype(BF16)).astype(F32)
    by_mean = jnp.sum(da * wide, -1, keepdims=True) * (-1.0 / D) * (scale * scale * scale)
    dh = dy + (da * scale + by_mean * wide).astype(BF16)
    dh_ref[...] = dh
    for j in range(n):
        at = pl.ds(j * CH, CH)
        back(gate0[:, at], up0[:, at], dot(dh, wd[0, at, :], NT_), dg0_ref, du0_ref, at)


def activations(x, dy, w_gate, w_up, w_down, T=256, CH=512):
    row = lambda w: pl.BlockSpec((T, w), lambda i: (i, 0))
    widths = (D, FF, FF, FF, D, FF, FF, FF, D)
    return pl.pallas_call(
        functools.partial(activations_kernel, CH),
        name="activations",
        grid=(S // T,),
        in_specs=[row(D), row(D), ANY, ANY, ANY],
        out_specs=[row(w) for w in widths],
        out_shape=[jax.ShapeDtypeStruct((S, w), BF16) for w in widths],
        scratch_shapes=[pltpu.VMEM((2, D, FF), BF16), pltpu.VMEM((2, D, FF), BF16), pltpu.VMEM((2, FF, D), BF16), pltpu.VMEM((T, FF), F32), pltpu.VMEM((T, FF), F32),
                        pltpu.SemaphoreType.DMA((2, 3))],
        cost_estimate=pl.CostEstimate(flops=18 * S * D * FF, bytes_accessed=2 * S * (6 * FF + 5 * D) + 12 * D * FF, transcendentals=2 * S * FF),
        compiler_params=pltpu.CompilerParams(vmem_limit_bytes=63 * 2**20),
    )(x, dy, w_gate, w_up, w_down)


def adamw_kernel(transposed, k, ss_ref, g_ref, w_ref, m_ref, v_ref, wo, mo, vo):
    total = jnp.sum(ss_ref[...], keepdims=True)
    f = jnp.minimum(1.0, 0.5 * lax.rsqrt(total / (6 * D * FF) + 1e-30))
    def part(g, r, c):
        g = g.astype(F32) * f
        m = 0.9 * m_ref[0, r, c] + 0.1 * g
        v = 0.95 * v_ref[0, r, c] + 0.05 * g * g
        w = w_ref[0, r, c].astype(F32)
        mo[0, r, c] = m
        vo[0, r, c] = v
        wo[0, r, c] = (w - 0.02 * (m * lax.rsqrt(v + 1e-8) + 0.1 * w)).astype(BF16)
    if not transposed:
        @pl.loop(0, 56)
        def _(r):
            for j in range(k):
                part(g_ref[0, j * 56 + r], pl.ds(pl.multiple_of(r * 16, 16), 16), slice(j * 128, (j + 1) * 128))
    else:
        @pl.loop(0, 7)
        def _(r):
            for j in range(k):
                t = g_ref[0, pl.ds(j * 56 + r * 8, 8)].reshape(128, 128).T
                part(t, slice(j * 128, (j + 1) * 128), pl.ds(pl.multiple_of(r * 128, 128), 128))


def adamw(transposed, which, ss, g, w, m, v, k=5):
    if transposed:
        spec = pl.BlockSpec((1, 128 * k, D), lambda l, i: (l, i, 0))
    else:
        spec = pl.BlockSpec((1, D, 128 * k), lambda l, i: (l, 0, i))
    gspec = pl.BlockSpec((1, 56 * k, 16, 128), lambda l, i: (which - 3 * l, i, 0, 0))
    n = w.size
    return pl.pallas_call(functools.partial(adamw_kernel, transposed, k), name="adamw", grid=(2, 20 // k),
        in_specs=[pl.BlockSpec((8, 128), lambda l, i: (0, 0)), gspec, spec, spec, spec], out_specs=[spec] * 3,
        out_shape=[jax.ShapeDtypeStruct(w.shape, BF16), jax.ShapeDtypeStruct(w.shape, F32), jax.ShapeDtypeStruct(w.shape, F32)],
        cost_estimate=pl.CostEstimate(flops=20 * n, bytes_accessed=22 * n, transcendentals=n),
        compiler_params=pltpu.CompilerParams(vmem_limit_bytes=48 * 2**20))(ss, g, w, m, v)


class Geo:
    def __init__(self, c):
        self.c = c
        self.p, self.q, self.r = COLORS[c]
        self.n, self.nq, self.nr = (SIZE[a] for a in COLORS[c])
        self.h = self.n // 2
        self.C = SLAB // self.n
        self.H = self.C // 2
        self.Cq = self.C // self.nq
        assert self.Cq == 3 * self.nr
        self.own = 2 * self.H + 2 * self.C * (self.h - 2) + self.C
        self.p2 = 2 * self.H + 2 * self.C * (self.h - 1)
        self.p3 = self.p2 + (self.nq - 1) * self.Cq
        assert self.p3 + 3 * (self.nr - 1) == RECV

    def L(self, s):
        return 2 * self.H + (s - 2) * 2 * self.C

    def R(self, s):
        return self.L(s) + self.C

    def own_step(self, s):
        return 2 * self.H + (s - 3) * 2 * self.C

    @property
    def own_mine(self):
        return 2 * self.H + 2 * self.C * (self.h - 2)


GEO = [Geo(c) for c in range(3)]
OWN = max(g.own for g in GEO)
RING = 4


def add_loop(n, body, unroll):
    assert n % unroll == 0
    if n == unroll:
        body(0, unroll)
    else:
        pl.loop(0, n // unroll)(lambda i: body(i * unroll, unroll))


class Comm:
    def __init__(self, g, out, recv, own, own1, own2, fin, sems):
        self.g, self.out, self.recv, self.own, self.own1, self.own2, self.fin = g, out, recv, own, own1, own2, fin
        (self.s_rs, self.s_ag, self.s_own, self.s_a, self.s_b, self.s_l, self.s_r, self.s_p2, self.s_p3, self.s_loc,
         self.s_gr, self.s_gq, self.s_gl, self.s_gright) = sems
        me = lax.axis_index("dp")
        self.me = me
        self.at = {"x": me // 32, "y": me // 8 % 4, "z": me % 8}

    def shift(self, ax, d):
        return lax.rem(self.at[ax] + (d + SIZE[ax]), SIZE[ax])

    def peer(self, ax, d):
        return {"dp": self.me + (self.shift(ax, d) - self.at[ax]) * STRIDE[ax]}

    def barrier(self):
        b = pltpu.get_barrier_semaphore()
        count = 0
        for ax in "xyz":
            for d in range(1, SIZE[ax]):
                pl.semaphore_signal(b, inc=1, device_id=self.peer(ax, d), device_id_type=MESH)
                count += 1
        pl.semaphore_wait(b, count)

    def send(self, src, dst, ssem, rsem, ax, d):
        pltpu.make_async_remote_copy(src_ref=src, dst_ref=dst, send_sem=ssem, recv_sem=rsem, device_id=self.peer(ax, d), device_id_type=MESH).start()

    def wait(self, ref, n, sem):
        pltpu.make_async_copy(ref.at[pl.ds(0, n)], ref.at[pl.ds(0, n)], sem).wait()

    def got(self, m, c, n, sem):
        self.wait(self.recv.at[m, c], n, sem)

    def raw(self, m, c):
        G = GEO[c]
        g, rv = self.g.at[m], self.recv.at[m, c]
        chunk = lambda d: c * SLAB + self.shift(G.p, d) * G.C
        ss = self.s_rs.at[m, c]
        self.send(g.at[pl.ds(chunk(G.h), G.H)], rv.at[pl.ds(0, G.H)], ss, self.s_a.at[m, c], G.p, 1)
        self.send(g.at[pl.ds(chunk(G.h) + G.H, G.H)], rv.at[pl.ds(G.H, G.H)], ss, self.s_b.at[m, c], G.p, -1)
        self.send(g.at[pl.ds(chunk(G.h - 1) + G.H, G.H)], rv.at[pl.ds(G.L(2) + G.H, G.H)], ss, self.s_l.at[m, c, 0], G.p, 1)
        self.send(g.at[pl.ds(chunk(1 - G.h), G.H)], rv.at[pl.ds(G.R(2), G.H)], ss, self.s_r.at[m, c, 0], G.p, -1)

    def load(self, m, c):
        G = GEO[c]
        g, own = self.g.at[m], self.own.at[m % RING, c]
        chunk = lambda d: c * SLAB + self.shift(G.p, d) * G.C
        parts = [(chunk(G.h - 1), 0, G.H), (chunk(1 - G.h) + G.H, G.H, G.H)]
        for s in range(3, G.h + 1):
            parts += [(chunk(G.h - s + 1), G.own_step(s), G.C), (chunk(s - G.h - 1), G.own_step(s) + G.C, G.C)]
        parts += [(chunk(0), G.own_mine, G.C)]
        for src, dst, n in parts:
            pltpu.make_async_copy(g.at[pl.ds(src, n)], own.at[pl.ds(dst, n)], self.s_own.at[m, c]).start()

    def add_in(self, m, c, at, own_at, n):
        rv, own = self.recv.at[m, c], self.own.at[m % RING, c]

        def body(i, k):
            rv[pl.ds(at + i, k)] = (rv[pl.ds(at + i, k)].astype(F32) + own[pl.ds(own_at + i, k)].astype(F32)).astype(BF16)

        add_loop(n, body, 8)

    def step(self, m, c, s):
        G = GEO[c]
        rv = self.recv.at[m, c]
        ss = self.s_rs.at[m, c]
        if s == 2:
            self.wait(self.own.at[m % RING, c], G.own, self.s_own.at[m, c])
            self.got(m, c, G.H, self.s_a.at[m, c])
            self.add_in(m, c, 0, 0, G.H)
            self.got(m, c, G.H, self.s_b.at[m, c])
            self.send(rv.at[pl.ds(0, G.H)], rv.at[pl.ds(G.L(2), G.H)], ss, self.s_l.at[m, c, 0], G.p, 1)
            self.add_in(m, c, G.H, G.H, G.H)
            self.send(rv.at[pl.ds(G.H, G.H)], rv.at[pl.ds(G.R(2) + G.H, G.H)], ss, self.s_r.at[m, c, 0], G.p, -1)
        else:
            self.got(m, c, G.C, self.s_l.at[m, c, s - 3])
            self.add_in(m, c, G.L(s - 1), G.own_step(s), G.C)
            self.got(m, c, G.C, self.s_r.at[m, c, s - 3])
            self.send(rv.at[pl.ds(G.L(s - 1), G.C)], rv.at[pl.ds(G.L(s), G.C)], ss, self.s_l.at[m, c, s - 2], G.p, 1)
            self.add_in(m, c, G.R(s - 1), G.own_step(s) + G.C, G.C)
            self.send(rv.at[pl.ds(G.R(s - 1), G.C)], rv.at[pl.ds(G.R(s), G.C)], ss, self.s_r.at[m, c, s - 2], G.p, -1)

    def first(self, m, c):
        G = GEO[c]
        rv, own = self.recv.at[m, c], self.own.at[m % RING, c]
        l, r, mine = G.L(G.h), G.R(G.h), G.own_mine
        self.got(m, c, G.C, self.s_l.at[m, c, G.h - 2])
        self.got(m, c, G.C, self.s_r.at[m, c, G.h - 2])

        def total(i, k):
            return own[pl.ds(mine + i, k)].astype(F32) + rv[pl.ds(l + i, k)].astype(F32) + rv[pl.ds(r + i, k)].astype(F32)

        keep = self.at[G.q] * G.Cq

        def body0(i, k):
            self.own1[m % RING, c, pl.ds(i, k)] = total(keep + i, k)

        def body1(i, k):
            rv[pl.ds(l + i, k)] = total(i, k).astype(BF16)

        add_loop(G.Cq, body0, 4)
        add_loop(G.C, body1, 8)
        for d in range(1, G.nq):
            self.send(rv.at[pl.ds(l + self.shift(G.q, d) * G.Cq, G.Cq)], rv.at[pl.ds(G.p2 + (d - 1) * G.Cq, G.Cq)],
                      self.s_rs.at[m, c], self.s_p2.at[m, c], G.q, d)

    def second(self, m, c):
        G = GEO[c]
        rv = self.recv.at[m, c]
        self.got(m, c, (G.nq - 1) * G.Cq, self.s_p2.at[m, c])

        def total(i, k):
            t = self.own1[m % RING, c, pl.ds(i, k)]
            for d in range(G.nq - 1):
                t = t + rv[pl.ds(G.p2 + d * G.Cq + i, k)].astype(F32)
            return t

        self.own2[m % RING, c] = total(self.at[G.r] * 3, 3)

        def body(i, k):
            rv[pl.ds(G.p2 + i, k)] = total(i, k).astype(BF16)

        add_loop(G.Cq, body, 4)
        for d in range(1, G.nr):
            self.send(rv.at[pl.ds(G.p2 + self.shift(G.r, d) * 3, 3)], rv.at[pl.ds(G.p3 + (d - 1) * 3, 3)],
                      self.s_rs.at[m, c], self.s_p3.at[m, c], G.r, d)

    def third(self, m, c):
        G = GEO[c]
        rv = self.recv.at[m, c]
        self.got(m, c, (G.nr - 1) * 3, self.s_p3.at[m, c])
        t = self.own2[m % RING, c]
        for d in range(G.nr - 1):
            t = t + rv[pl.ds(G.p3 + 3 * d, 3)].astype(F32)
        t = t.astype(BF16)
        self.fin[m, c] = t
        t = t.astype(F32)
        return jnp.sum((t * t).reshape(6, 8, 128), axis=0)

    def rs_sent(self, m, c):
        G = GEO[c]
        n = 4 * G.H + 2 * G.H + 2 * G.C * (G.h - 2) + (G.nq - 1) * G.Cq + (G.nr - 1) * 3
        self.wait(self.g.at[m], n, self.s_rs.at[m, c])

    def place(self, c, p, q=None, r=None):
        G = GEO[c]
        return c * SLAB + p * G.C + (0 if q is None else q * G.Cq) + (0 if r is None else r * 3)

    def gather_r(self, m, c):
        G = GEO[c]
        at = pl.ds(self.place(c, self.at[G.p], self.at[G.q], self.at[G.r]), 3)
        dst = self.out.at[m, at]
        for d in range(1, G.nr):
            self.send(self.fin.at[m, c], dst, self.s_ag.at[m, c], self.s_gr.at[m, c], G.r, d)
        pltpu.make_async_copy(self.fin.at[m, c], dst, self.s_loc.at[m, c]).start()

    def gather_q(self, m, c):
        G = GEO[c]
        self.wait(self.out.at[m], 3, self.s_loc.at[m, c])
        self.wait(self.out.at[m], 3 * (G.nr - 1), self.s_gr.at[m, c])
        ref = self.out.at[m, pl.ds(self.place(c, self.at[G.p], self.at[G.q]), G.Cq)]
        for d in range(1, G.nq):
            self.send(ref, ref, self.s_ag.at[m, c], self.s_gq.at[m, c], G.q, d)

    def gather_p(self, m, c, s):
        G = GEO[c]
        if s == 1:
            self.wait(self.out.at[m], (G.nq - 1) * G.Cq, self.s_gq.at[m, c])
        else:
            self.wait(self.out.at[m], G.C, self.s_gl.at[m, c, s - 2])
            self.wait(self.out.at[m], G.C, self.s_gright.at[m, c, s - 2])
        n = G.C if s < G.h else G.H
        a = self.out.at[m, pl.ds(self.place(c, self.shift(G.p, 1 - s)), n)]
        b = self.out.at[m, pl.ds(self.place(c, self.shift(G.p, s - 1)) + (G.C - n), n)]
        self.send(a, a, self.s_ag.at[m, c], self.s_gl.at[m, c, s - 1], G.p, 1)
        self.send(b, b, self.s_ag.at[m, c], self.s_gright.at[m, c, s - 1], G.p, -1)

    def gathered(self, m, c):
        G = GEO[c]
        self.wait(self.out.at[m], G.H, self.s_gl.at[m, c, G.h - 1])
        self.wait(self.out.at[m], G.H, self.s_gright.at[m, c, G.h - 1])
        n = 3 * (G.nr - 1) + (G.nq - 1) * G.Cq + 2 * G.C * (G.h - 1) + 2 * G.H
        self.wait(self.g.at[m], n, self.s_ag.at[m, c])


def comm_scratch(k):
    dma = pltpu.SemaphoreType.DMA
    return [
        pltpu.VMEM((k, 3, RECV) + TILE, BF16),
        pltpu.VMEM((RING, 3, OWN) + TILE, BF16),
        pltpu.VMEM((RING, 3, 24) + TILE, F32),
        pltpu.VMEM((RING, 3, 3) + TILE, F32),
        pltpu.VMEM((k, 3, 3) + TILE, BF16),
    ], [dma((k, 3)), dma((k, 3)), dma((k, 3)), dma((k, 3)), dma((k, 3)), dma((k, 3, 3)), dma((k, 3, 3)), dma((k, 3)), dma((k, 3)), dma((k, 3)),
        dma((k, 3)), dma((k, 3)), dma((k, 3, 4)), dma((k, 3, 4))]


def norm_exchange(comm, acc, slots, s_send, s_recv):
    first, total = 0, acc[...]
    for i, ax in enumerate("xyz"):
        n = SIZE[ax]
        slots[pl.ds(first + comm.at[ax], 1)] = total[None]
        ref = slots.at[pl.ds(first + comm.at[ax], 1)]
        for d in range(1, n):
            comm.send(ref, ref, s_send.at[i], s_recv.at[i], ax, d)
        yield
        comm.wait(slots, n - 1, s_recv.at[i])
        total = slots[first]
        for k in range(1, n):
            total = total + slots[first + k]
        first += n
    yield total
    for i, ax in enumerate("xyz"):
        comm.wait(slots, SIZE[ax] - 1, s_send.at[i])


STEPS = FF // 512


def schedule(k):
    ev = []
    for m in range(k):
        for c in range(3):
            for name, t in event_times(m, c, GEO[c].h):
                ev.append((t, len(ev), m, c, name))
    last = max(e[0] for e in ev if e[4] == "third")
    for i, t in enumerate((0.2, 5, 10, 16)):
        ev.append((last + t, len(ev), k, 0, f"norm{i}"))
    ev.sort()
    order = [(e[2], e[3], e[4]) for e in ev]
    for m in range(k):
        for c in range(3):
            names = [e[2] for e in order if e[:2] == (m, c)]
            assert names == [name for name, _ in event_times(m, c, GEO[c].h)], names
    for m in range(k - RING):
        for c in range(3):
            assert order.index((m, c, "first")) < order.index((m + RING, c, "raw"))
            assert order.index((m, c, "third")) < order.index((m + RING, c, "first"))
    return [(t / STEP, m, c, name) for t, _, m, c, name in ev]


def event_times(m, c, h):
    b = STEP * 5 * (m + 1) + PACE * m
    yield "raw", STEP * (5 * m + 4 - 0.5 if c == 0 else 5 * m + 5 - 0.01)
    if c < 2:
        yield "step2", b + RS * 12
    else:
        for s in range(2, h + 1):
            yield f"step{s}", b + RS * (8 + 4 * (s - 2))
    yield "first", b + RS * 20
    yield "second", b + RS * 26
    yield "third", b + RS * 31
    b += RS * 31 + AGX
    yield "gather1", b + 0.1
    yield "gather2", b + AG * 5
    for s in range(1, h + 1):
        yield f"along{s}", b + AG * (11 + (s - 1) * 20 / h)
    yield "end", 10000


STEP = 2.4
PACE = 0
RS = 1
AG = 1
AGX = 0


def gradients_kernel(k, pairs, *refs):
    nl = len(set(pairs))
    lefts, rights = refs[:6], refs[6:12]
    g, out, ss_out, recv, own, own1, own2, fin, acc, slots, lbuf, rbuf, obuf, zero = refs[12:26]
    sems = refs[26:]
    comm = Comm(g, out, recv, own, own1, own2, fin, sems[:14])
    s_send, s_recv, s_left, s_right, s_out, s_zero = sems[14:]
    comm.barrier()
    acc[...] = jnp.zeros_like(acc)
    zero[...] = jnp.zeros_like(zero)

    def left(m):
        return pltpu.make_async_copy(lefts[m], lbuf.at[m % 2], s_left.at[m % 2])

    def right(m, j):
        slot = (m * STEPS + j) % 2
        return pltpu.make_async_copy(rights[m].at[:, pl.ds(j * 512, 512)], rbuf.at[slot], s_right.at[slot])

    def put(m, j):
        slot = (m * STEPS + j) % 2
        return pltpu.make_async_copy(obuf.at[slot], g.at[m, pl.ds(j * 224, 224)], s_out.at[slot])

    def blank(m):
        return pltpu.make_async_copy(zero, g.at[m, pl.ds(1120, 32)], s_zero.at[m])

    left(0).start()
    right(0, 0).start()
    for m in range(k):
        blank(m).start()
    for m in range(k):
        blank(m).wait()

    def last(e):
        return e[3] == "raw" and e[2] > 0

    norm = norm_exchange(comm, acc, slots, s_send, s_recv)

    def run(m, c, name):
        if name.startswith("norm"):
            total = next(norm)
            if name == "norm3":
                ss_out[...] = total
                for _ in norm:
                    pass
        elif name == "raw":
            comm.raw(m, c)
            comm.load(m, c)
        elif name.startswith("step"):
            comm.step(m, c, int(name[4:]))
        elif name == "third":
            acc[...] += comm.third(m, c)
        elif name == "gather1":
            comm.gather_r(m, c)
        elif name == "gather2":
            comm.gather_q(m, c)
        elif name.startswith("along"):
            comm.gather_p(m, c, int(name[5:]))
        elif name == "end":
            comm.rs_sent(m, c)
            comm.gathered(m, c)
        else:
            getattr(comm, name)(m, c)

    events = schedule(k)
    for m in range(k):
        left(m).wait()

        @pl.loop(0, STEPS)
        def _(j):
            right(m, j).wait()

            @pl.when(j < STEPS - 1)
            def _():
                right(m, j + 1).start()

            if m + 1 < k:
                @pl.when(j == STEPS - 1)
                def _():
                    right(m + 1, 0).start()

                @pl.when(j == 1)
                def _():
                    left(m + 1).start()

            @pl.when(j >= 2)
            def _():
                put(m, j - 2).wait()

            slot = (m * STEPS + j) % 2
            v = dot(lbuf[m % 2], rbuf[slot], TN).astype(BF16)
            for c in range(4):
                obuf[slot, c * 56:(c + 1) * 56] = v[:, c * 128:(c + 1) * 128].reshape((56,) + TILE)
            put(m, j).start()
            for n in range(STEPS):
                now = [e[1:] for e in events if int(e[0]) == STEPS * m + n and not last(e)]
                if now:
                    @pl.when(j == n)
                    def _():
                        for e in now:
                            run(*e)

        put(m, STEPS - 2).wait()
        put(m, STEPS - 1).wait()
        for e in events:
            if int(e[0]) == STEPS * m + STEPS - 1 and last(e):
                run(*e[1:])
    for e in events:
        if e[0] >= STEPS * k:
            run(*e[1:])


def gradients(x, dy, w_gate, w_up, w_down):
    a0, z0, dg0, du0, a1, z1, dg1, du1, dh = activations(x, dy, w_gate, w_up, w_down, CH=256)
    return (dy, a1, a1, dh, a0, a0), (z1, dg1, du1, z0, dg0, du0)


def summed(lefts, rights):
    k = 6
    bufs, sems = comm_scratch(k)
    dma = pltpu.SemaphoreType.DMA
    return pl.pallas_call(
        functools.partial(gradients_kernel, k, tuple(range(6))),
        name="gradients",
        out_shape=(jax.ShapeDtypeStruct((k, NT) + TILE, BF16), jax.ShapeDtypeStruct((k, NT) + TILE, BF16), jax.ShapeDtypeStruct((8, 128), F32)),
        in_specs=[ANY] * 12,
        out_specs=(ANY, ANY, pl.BlockSpec(memory_space=pltpu.VMEM)),
        scratch_shapes=bufs + [pltpu.VMEM((8, 128), F32), pltpu.VMEM((16, 8, 128), F32),
                               pltpu.VMEM((2, S, D), BF16), pltpu.VMEM((2, S, 512), BF16), pltpu.VMEM((2, 224) + TILE, BF16), pltpu.VMEM((32,) + TILE, BF16)]
        + sems + [dma((3,)), dma((3,)), dma((2,)), dma((2,)), dma((2,)), dma((k,))],
        cost_estimate=pl.CostEstimate(flops=12 * S * D * FF, bytes_accessed=12 * S * (D + FF), transcendentals=0),
        compiler_params=pltpu.CompilerParams(collective_id=0, has_side_effects=True, vmem_limit_bytes=67043328),
    )(*lefts, *rights)


def solution(mesh):
    def step(x, dy, w_gate, w_up, w_down, m_gate, m_up, m_down, v_gate, v_up, v_down):
        _, g, ss = summed(*gradients(x[0], dy[0], w_gate, w_up, w_down))
        new = [
            adamw(False, 4, ss, g, w_gate, m_gate, v_gate),
            adamw(False, 5, ss, g, w_up, m_up, v_up),
            adamw(True, 3, ss, g, w_down, m_down, v_down),
        ]
        return tuple(one[which] for which in range(3) for one in new)

    return jax.shard_map(
        step,
        mesh=mesh,
        in_specs=(P(("rep", "dp"), None, None),) * 2 + (P(None, None, None),) * 9,
        out_specs=(P("rep", None, None),) * 9,
        check_vma=False,
    )
```

time: 917 us -> 505 us (0.55)
  Pallas kernels: 0 us -> 503 us
  waiting for transfers between devices: 456 us -> 0 us
  matrix products: 285 us -> 0 us
  other arithmetic: 137 us -> 0 us
  between operations: 16.6 us -> 0.67 us
  local copies, waits for them, and re-layouts: 14.2 us -> 0.67 us
    pallas_call x0 -> x5, Pallas kernels: none -> 503 us  [the longest x1 275 us: summed(): pl.pallas_call(functools.partial(gradients_kernel, k, tuple(range(6))), n...]
    psum x1 -> x0, waiting for transfers between devices: 456 us -> none  [step(): summed[number] = [lax.psum(by_w[name], 'dp') for name in NAMES]]
    dot_general x15 -> x0, matrix products: 285 us -> none  [the longest x5 103 us: layer(): gate = jnp.dot(a, w['w_gate'], preferred_element_type=jnp.float32)]
    convert_element_type x2 -> x0, other arithmetic: 103 us -> none  [adamw(): return ((w - 0.02 * step).astype(jnp.bfloat16), m, v)]
    reduce_sum x4 -> x0, other arithmetic: 26.3 us -> none  [the longest x3 23.5 us: step(): jnp.sum(g * g)]
    unnamed x38 -> x2, local copies, waits for them, and re-layouts: 14.2 us -> 0.67 us
  transfers between devices with their start and end apart: 1 -> 0, of which waited for: 1 -> 0; matrix products, arithmetic and copies ran while one was open for 0% -> 0% of each run, Pallas kernels for 0% -> 0%
where the time goes in v1:
time: 505 us; the launch traced here: 504 us
  Pallas kernels  503 us (100%)
    pallas_call x1, Pallas kernels, summed(): pl.pallas_call(functools.partial(gradients_kernel, k, tuple(range(6))), n...  275 us
    pallas_call x1, Pallas kernels, activations(): pl.pallas_call(functools.partial(activations_kernel, CH), name='activatio...  118 us
    pallas_call x3, Pallas kernels, adamw(): pl.pallas_call(functools.partial(adamw_kernel, transposed, k), name='adam...  110 us

profile of v1, /device:TPU:2, one launch (start us, length us, event | category | flops | bytes accessed | tf_op | source)
XLA Modules:
  0.0 504.4 jit_solution(1556872543450772900)
XLA Ops:
  0.6 117.5 %activations.1 = (bf16[2048,896]{1,0:T(8,128)(2,1)}, bf16[2048,2560]{1,0:T(8,128)(2,1)}, bf16[2048,2560]{1,0:T(8,128)(2,1)}, bf16[2048,2560]{1,0:T(8,128)(2,1)},...) custom-call(bf16[2048,896]{1,0:T(8,128)(2,1)} %bitcast.2, ...), custom_call_target="tpu_custom_call" | custom-call | flops 84557168640 | bytes 108789760 | tf_op jit(solution)/shard_map/activations/pallas_call | solution.py:98
  118.2 275.4 %gradients.1 = (bf16[6,1152,16,128]{3,2,1,0:T(8,128)(2,1)}, bf16[6,1152,16,128]{3,2,1,0:T(8,128)(2,1)}, f32[8,128]{1,0:T(8,128)}) custom-call(bf16[2048,896]{1,0:T(8,128)(2,1)} %bitcast.4, bf16[2048,896]{1,0:T(8,128)(2,1)} %get-tuple-element.29.refs_1_.refs_2_, bf16[2048,896]{1,0:T(8,128)(2,1)} %get-tuple-element.29.refs_1_.refs_2_, ...), custom_call_target="tpu_custom_call" | custom-call | flops 56371445760 | bytes 84934656 | tf_op jit(solution)/shard_map/gradients/pallas_call | solution.py:579
  393.6 0.0 copy-start
  393.6 0.7 copy-done
  394.3 36.1 %adamw.5 = (bf16[2,2560,896]{2,1,0:T(8,128)(2,1)}, f32[2,2560,896]{2,1,0:T(8,128)}, f32[2,2560,896]{2,1,0:T(8,128)}) custom-call(f32[8,128]{1,0:T(8,128)S(1)} %copy-done, bf16[6,1152,16,128]{3,2,1,0:T(8,128)(2,1)} %get-tuple-element.39.g_ref, bf16[2,2560,896]{2,1,0:T(8,128)(2,1)} %w_ref.5, f32[2,2560,896]{2,1,0:T(8,128)} %m_ref.5, f32[2,2560,896]{2,1,0:T(8,128)} %v_ref.5), custom_call_target="tpu_custom_call" | custom-call | flops 91750400 | bytes 100925440 | tf_op jit(solution)/shard_map/adamw/pallas_call | solution.py:143
  430.4 37.0 %adamw.4 = (bf16[2,896,2560]{2,1,0:T(8,128)(2,1)}, f32[2,896,2560]{2,1,0:T(8,128)}, f32[2,896,2560]{2,1,0:T(8,128)}) custom-call(f32[8,128]{1,0:T(8,128)S(1)} %copy-done, bf16[6,1152,16,128]{3,2,1,0:T(8,128)(2,1)} %get-tuple-element.39.g_ref, bf16[2,896,2560]{2,1,0:T(8,128)(2,1)} %w_ref.4, f32[2,896,2560]{2,1,0:T(8,128)} %m_ref.4, f32[2,896,2560]{2,1,0:T(8,128)} %v_ref.4), custom_call_target="tpu_custom_call" | custom-call | flops 91750400 | bytes 100925440 | tf_op jit(solution)/shard_map/adamw/pallas_call | solution.py:143
  467.4 37.0 %adamw.3 = (bf16[2,896,2560]{2,1,0:T(8,128)(2,1)}, f32[2,896,2560]{2,1,0:T(8,128)}, f32[2,896,2560]{2,1,0:T(8,128)}) custom-call(f32[8,128]{1,0:T(8,128)S(1)} %copy-done, bf16[6,1152,16,128]{3,2,1,0:T(8,128)(2,1)} %get-tuple-element.39.g_ref, bf16[2,896,2560]{2,1,0:T(8,128)(2,1)} %w_ref.3, f32[2,896,2560]{2,1,0:T(8,128)} %m_ref.3, f32[2,896,2560]{2,1,0:T(8,128)} %v_ref.3), custom_call_target="tpu_custom_call" | custom-call | flops 91750400 | bytes 100925440 | tf_op jit(solution)/shard_map/adamw/pallas_call | solution.py:143
Async XLA Ops:
  393.6 0.7 copy-start

commit v2 on v1

v2 whole, which is shorter than its diff:
```python
import functools

import jax
import jax.numpy as jnp
from jax import lax
from jax.experimental import pallas as pl
from jax.experimental.pallas import tpu as pltpu
from jax.sharding import PartitionSpec as P

F32, BF16 = jnp.float32, jnp.bfloat16
S, D, FF = 2048, 896, 2560
MESH = pl.DeviceIdType.MESH
ANY = pl.BlockSpec(memory_space=pl.ANY)
TILE = (16, 128)
NT = 1152
SLAB = 384
SQUARES = (8, 128)
ROOM, MOST = 63 * 2**20, 67043328
THREE = range(3)
SHARE = 3
LANES, BANDS = 128, 56
SIZE = {"x": 4, "y": 4, "z": 8}
STRIDE = {"x": 32, "y": 8, "z": 1}
COLORS = ((("x", "y", "z"), ("y", "x", "z"), ("z", "x", "y")), (("x", "y", "z"), ("y", "x", "z"), ("z", "y", "x")))
RECV = 381
NN = (((1,), (0,)), ((), ()))
NT_ = (((1,), (1,)), ((), ()))
TN = (((0,), (0,)), ((), ()))


def dot(a, b, dims=NN):
    return lax.dot_general(a, b, dims, preferred_element_type=F32)


def sigmoid(x):
    return 0.5 + 0.5 * jnp.tanh(0.5 * x)


def norm_of(h):
    wide = h.astype(F32)
    return wide, lax.rsqrt(jnp.mean(wide * wide, -1, keepdims=True) + 1e-6)


def activations_kernel(CH, x_ref, dy_ref, wg_hbm, wu_hbm, wd_hbm, a0_ref, z0_ref, dg0_ref, du0_ref, a1_ref, z1_ref, dg1_ref, du1_ref, dh_ref, wg, wu, wd, gate0, up0, sem):
    first = pl.program_id(0) == 0
    n = FF // CH
    copies = [[pltpu.make_async_copy(hbm.at[layer], vmem.at[layer], sem.at[layer, k]) for k, (hbm, vmem) in enumerate(((wg_hbm, wg), (wu_hbm, wu), (wd_hbm, wd)))] for layer in range(2)]

    @pl.when(first)
    def _():
        for layer in range(2):
            for copy in copies[layer]:
                copy.start()
        copies[0][0].wait()
        copies[0][1].wait()

    x = x_ref[...]
    dy = dy_ref[...]
    wide, scale = norm_of(x)
    a = (wide * scale).astype(BF16)
    a0_ref[...] = a
    for j in range(n):
        at = pl.ds(j * CH, CH)
        gate, up = dot(a, wg[0, :, at]), dot(a, wu[0, :, at])
        gate0[:, at] = gate
        up0[:, at] = up
        z0_ref[:, at] = (gate * sigmoid(gate) * up).astype(BF16)

    @pl.when(first)
    def _():
        copies[0][2].wait()

    h = x + dot(z0_ref[...], wd[0]).astype(BF16)
    wide, scale = norm_of(h)
    a = (wide * scale).astype(BF16)
    a1_ref[...] = a

    @pl.when(first)
    def _():
        for copy in copies[1]:
            copy.wait()

    def back(gate, up, dz, dg_ref, du_ref, at):
        dz = dz.astype(BF16).astype(F32)
        sig = sigmoid(gate)
        silu = gate * sig
        du_ref[:, at] = (dz * silu).astype(BF16)
        dg_ref[:, at] = (dz * up * (sig + silu * (1.0 - sig))).astype(BF16)
        return silu

    for j in range(n):
        at = pl.ds(j * CH, CH)
        gate, up, dz = dot(a, wg[1, :, at]), dot(a, wu[1, :, at]), dot(dy, wd[1, at, :], NT_)
        z1_ref[:, at] = (back(gate, up, dz, dg1_ref, du1_ref, at) * up).astype(BF16)
    da = (dot(dg1_ref[...], wg[1], NT_).astype(BF16) + dot(du1_ref[...], wu[1], NT_).astype(BF16)).astype(F32)
    by_mean = jnp.sum(da * wide, -1, keepdims=True) * (-1.0 / D) * (scale * scale * scale)
    dh = dy + (da * scale + by_mean * wide).astype(BF16)
    dh_ref[...] = dh
    for j in range(n):
        at = pl.ds(j * CH, CH)
        back(gate0[:, at], up0[:, at], dot(dh, wd[0, at, :], NT_), dg0_ref, du0_ref, at)


def activations(x, dy, w_gate, w_up, w_down, T=256, CH=512):
    row = lambda w: pl.BlockSpec((T, w), lambda i: (i, 0))
    widths = (D, FF, FF, FF, D, FF, FF, FF, D)
    return pl.pallas_call(
        functools.partial(activations_kernel, CH),
        name="activations",
        grid=(S // T,),
        in_specs=[row(D), row(D), ANY, ANY, ANY],
        out_specs=[row(w) for w in widths],
        out_shape=[jax.ShapeDtypeStruct((S, w), BF16) for w in widths],
        scratch_shapes=[pltpu.VMEM((2, D, FF), BF16), pltpu.VMEM((2, D, FF), BF16), pltpu.VMEM((2, FF, D), BF16), pltpu.VMEM((T, FF), F32), pltpu.VMEM((T, FF), F32),
                        pltpu.SemaphoreType.DMA((2, 3))],
        cost_estimate=pl.CostEstimate(flops=18 * S * D * FF, bytes_accessed=2 * S * (6 * FF + 5 * D) + 12 * D * FF, transcendentals=2 * S * FF),
        compiler_params=pltpu.CompilerParams(vmem_limit_bytes=ROOM),
    )(x, dy, w_gate, w_up, w_down)


NB = 2


def adamw_kernel(B, ss_ref, g_hbm, *refs):
    ins, outs = [refs[i:9:3] for i in THREE], [refs[9 + i:18:3] for i in THREE]
    gb, wb, mb, vb, wo, mo, vo = [refs[18 + 3 * i:21 + 3 * i] for i in range(7)]
    s_in, s_out = refs[39:]
    n = 20 // B
    total = jnp.sum(ss_ref[...], keepdims=True)
    f = jnp.minimum(1.0, 0.5 * lax.rsqrt(total / (6 * D * FF) + 1e-30))

    def block(ref, k, i):
        at = pl.ds(pl.multiple_of(i % n * (LANES * B), LANES * B), LANES * B)
        return ref.at[i // n, at, :] if k == 2 else ref.at[i // n, :, at]

    def loads(k, i):
        g = g_hbm.at[(4, 5, 3)[k] - 3 * (i // n), pl.ds(i % n * (BANDS * B), BANDS * B)]
        pairs = [(g, gb[k])] + [(block(h, k, i), v[k]) for h, v in zip(ins[k], (wb, mb, vb))]
        return [pltpu.make_async_copy(h, v.at[i % NB], s_in.at[k, i % NB, p]) for p, (h, v) in enumerate(pairs)]

    def stores(k, i):
        return [pltpu.make_async_copy(v[k].at[i % NB], block(h, k, i), s_out.at[k, i % NB, p]) for p, (h, v) in enumerate(zip(outs[k], (wo, mo, vo)))]

    def part(k, slot, g, r, c):
        g = g.astype(F32) * f
        m = 0.9 * mb[k][slot, r, c] + 0.1 * g
        v = 0.95 * vb[k][slot, r, c] + 0.05 * g * g
        w = wb[k][slot, r, c].astype(F32)
        wo[k][slot, r, c] = (w - 0.02 * (m * lax.rsqrt(v + 1e-8) + 0.1 * w)).astype(BF16)
        mo[k][slot, r, c] = m
        vo[k][slot, r, c] = v

    for i in range(NB):
        for k in THREE:
            for copy in loads(k, i):
                copy.start()

    @pl.loop(0, 2 * n)
    def _(i):
        slot = i % NB
        for k in THREE:
            for copy in loads(k, i):
                copy.wait()

            @pl.when(i >= NB)
            def _():
                for copy in stores(k, i - NB):
                    copy.wait()

            if k < 2:
                @pl.loop(0, BANDS)
                def _(r):
                    rows = pl.ds(pl.multiple_of(r * 16, 16), 16)
                    for j in range(B):
                        part(k, slot, gb[k][slot, j * BANDS + r], rows, slice(j * LANES, (j + 1) * LANES))
            else:
                @pl.loop(0, 7)
                def _(r):
                    for j in range(B):
                        g = gb[k][slot, pl.ds(j * BANDS + r * 8, 8)].reshape(LANES, LANES).T
                        part(k, slot, g, slice(j * LANES, (j + 1) * LANES), pl.ds(pl.multiple_of(r * LANES, LANES), LANES))

            for copy in stores(k, i):
                copy.start()

            @pl.when(i + NB < 2 * n)
            def _():
                for copy in loads(k, i + NB):
                    copy.start()

    for i in range(2 * n - NB, 2 * n):
        for k in THREE:
            for copy in stores(k, i):
                copy.wait()


def adamw(ss, g, w, m, v, B=4):
    n = 6 * D * FF
    shapes = ((NB, D, LANES * B), (NB, D, LANES * B), (NB, LANES * B, D))
    three = lambda t: [pltpu.VMEM(s, t) for s in shapes]
    return pl.pallas_call(
        functools.partial(adamw_kernel, B),
        name="adamw",
        in_specs=[pl.BlockSpec(memory_space=pltpu.VMEM)] + [ANY] * 10,
        out_specs=[ANY] * 9,
        out_shape=[jax.ShapeDtypeStruct(a.shape, t) for t in (BF16, F32, F32) for a in w],
        scratch_shapes=[pltpu.VMEM((NB, BANDS * B) + TILE, BF16)] * 3 + three(BF16) + three(F32) * 2 + three(BF16) + three(F32) * 2
        + [pltpu.SemaphoreType.DMA((3, NB, 4)), pltpu.SemaphoreType.DMA((3, NB, 3))],
        cost_estimate=pl.CostEstimate(flops=20 * n, bytes_accessed=22 * n, transcendentals=n),
        compiler_params=pltpu.CompilerParams(vmem_limit_bytes=ROOM),
    )(ss, g, *w, *m, *v)


class Geo:
    def __init__(self, c, axes):
        self.c = c
        self.p, self.q, self.r = axes
        self.n, self.nq, self.nr = (SIZE[a] for a in axes)
        self.h = self.n // 2
        self.C = SLAB // self.n
        self.H = self.C // 2
        self.Cq = self.C // self.nq
        assert self.Cq == 3 * self.nr
        self.long = self.nr == 8
        self.own = 2 * self.H + 2 * self.C * (self.h - 2) + self.C
        self.p2 = 2 * self.H + 2 * self.C * (self.h - 1)
        self.p3 = self.p2 + (self.nq - 1) * self.Cq
        assert self.p3 + 3 * (self.nr - 1) == RECV

    def L(self, s):
        return 2 * self.H + (s - 2) * 2 * self.C

    def R(self, s):
        return self.L(s) + self.C

    def own_step(self, s):
        return 2 * self.H + (s - 3) * 2 * self.C

    @property
    def own_mine(self):
        return 2 * self.H + 2 * self.C * (self.h - 2)


GEO = [[Geo(c, axes) for c, axes in enumerate(colors)] for colors in COLORS]


def geo(m, c):
    return GEO[m % 2][c]


OWN = max(g.own for g in GEO[0])
RING = 4


def add_loop(n, body, unroll):
    assert n % unroll == 0
    if n == unroll:
        body(0, unroll)
    else:
        pl.loop(0, n // unroll)(lambda i: body(i * unroll, unroll))


class Comm:
    def __init__(self, g, out, recv, own, own1, own2, fin, sems):
        self.g, self.out, self.recv, self.own, self.own1, self.own2, self.fin = g, out, recv, own, own1, own2, fin
        (self.s_rs, self.s_ag, self.s_own, self.s_a, self.s_b, self.s_l, self.s_r, self.s_p2, self.s_p3, self.s_loc,
         self.s_gr, self.s_gq, self.s_gl, self.s_gright, self.s_za, self.s_zg, self.s_qa, self.s_gh) = sems
        me = lax.axis_index("dp")
        self.me = me
        self.at = {"x": me // 32, "y": me // 8 % 4, "z": me % 8}
        self.even = lax.rem(me, 2) == 0
        self.way = 1 - 2 * lax.rem(me, 2)

    def shift(self, ax, d):
        return lax.rem(self.at[ax] + (d + SIZE[ax]), SIZE[ax])

    def peer(self, ax, d):
        return {"dp": self.me + (self.shift(ax, d) - self.at[ax]) * STRIDE[ax]}

    def barrier(self):
        b = pltpu.get_barrier_semaphore()
        count = 0
        for ax in "xyz":
            for d in range(1, SIZE[ax]):
                pl.semaphore_signal(b, inc=1, device_id=self.peer(ax, d), device_id_type=MESH)
                count += 1
        pl.semaphore_wait(b, count)

    def send(self, src, dst, ssem, rsem, ax, d):
        pltpu.make_async_remote_copy(src_ref=src, dst_ref=dst, send_sem=ssem, recv_sem=rsem, device_id=self.peer(ax, d), device_id_type=MESH).start()

    def wait(self, ref, n, sem):
        pltpu.make_async_copy(ref.at[pl.ds(0, n)], ref.at[pl.ds(0, n)], sem).wait()

    def got(self, m, c, n, sem):
        self.wait(self.recv.at[m, c], n, sem)

    def raw(self, m, c):
        G = geo(m, c)
        g, rv = self.g.at[m], self.recv.at[m, c]
        chunk = lambda d: c * SLAB + self.shift(G.p, d) * G.C
        ss = self.s_rs.at[m, c]
        self.send(g.at[pl.ds(chunk(G.h), G.H)], rv.at[pl.ds(0, G.H)], ss, self.s_a.at[m, c], G.p, 1)
        self.send(g.at[pl.ds(chunk(G.h) + G.H, G.H)], rv.at[pl.ds(G.H, G.H)], ss, self.s_b.at[m, c], G.p, -1)
        self.send(g.at[pl.ds(chunk(G.h - 1) + G.H, G.H)], rv.at[pl.ds(G.L(2) + G.H, G.H)], ss, self.s_l.at[m, c, 0], G.p, 1)
        self.send(g.at[pl.ds(chunk(1 - G.h), G.H)], rv.at[pl.ds(G.R(2), G.H)], ss, self.s_r.at[m, c, 0], G.p, -1)

    def load(self, m, c):
        G = geo(m, c)
        g, own = self.g.at[m], self.own.at[m % RING, c]
        chunk = lambda d: c * SLAB + self.shift(G.p, d) * G.C
        parts = [(chunk(G.h - 1), 0, G.H), (chunk(1 - G.h) + G.H, G.H, G.H)]
        for s in range(3, G.h + 1):
            parts += [(chunk(G.h - s + 1), G.own_step(s), G.C), (chunk(s - G.h - 1), G.own_step(s) + G.C, G.C)]
        parts += [(chunk(0), G.own_mine, G.C)]
        for src, dst, n in parts:
            pltpu.make_async_copy(g.at[pl.ds(src, n)], own.at[pl.ds(dst, n)], self.s_own.at[m, c]).start()

    def add_in(self, m, c, at, own_at, n):
        rv, own = self.recv.at[m, c], self.own.at[m % RING, c]

        def body(i, k):
            rv[pl.ds(at + i, k)] = (rv[pl.ds(at + i, k)].astype(F32) + own[pl.ds(own_at + i, k)].astype(F32)).astype(BF16)

        add_loop(n, body, 8)

    def step(self, m, c, s):
        G = geo(m, c)
        rv = self.recv.at[m, c]
        ss = self.s_rs.at[m, c]
        if s == 2:
            self.wait(self.own.at[m % RING, c], G.own, self.s_own.at[m, c])
            self.got(m, c, G.H, self.s_a.at[m, c])
            self.add_in(m, c, 0, 0, G.H)
            self.got(m, c, G.H, self.s_b.at[m, c])
            self.send(rv.at[pl.ds(0, G.H)], rv.at[pl.ds(G.L(2), G.H)], ss, self.s_l.at[m, c, 0], G.p, 1)
            self.add_in(m, c, G.H, G.H, G.H)
            self.send(rv.at[pl.ds(G.H, G.H)], rv.at[pl.ds(G.R(2) + G.H, G.H)], ss, self.s_r.at[m, c, 0], G.p, -1)
        else:
            self.got(m, c, G.C, self.s_l.at[m, c, s - 3])
            self.add_in(m, c, G.L(s - 1), G.own_step(s), G.C)
            self.got(m, c, G.C, self.s_r.at[m, c, s - 3])
            self.send(rv.at[pl.ds(G.L(s - 1), G.C)], rv.at[pl.ds(G.L(s), G.C)], ss, self.s_l.at[m, c, s - 2], G.p, 1)
            self.add_in(m, c, G.R(s - 1), G.own_step(s) + G.C, G.C)
            self.send(rv.at[pl.ds(G.R(s - 1), G.C)], rv.at[pl.ds(G.R(s), G.C)], ss, self.s_r.at[m, c, s - 2], G.p, -1)

    def first(self, m, c):
        G = geo(m, c)
        rv, own = self.recv.at[m, c], self.own.at[m % RING, c]
        l, r, mine = G.L(G.h), G.R(G.h), G.own_mine
        self.got(m, c, G.C, self.s_l.at[m, c, G.h - 2])
        self.got(m, c, G.C, self.s_r.at[m, c, G.h - 2])

        def total(i, k):
            return own[pl.ds(mine + i, k)].astype(F32) + rv[pl.ds(l + i, k)].astype(F32) + rv[pl.ds(r + i, k)].astype(F32)

        half = G.Cq // 2

        def keep(at, start, n):
            def body(i, k):
                self.own1[m % 2, c, pl.ds(at + i, k)] = total(start + i, k)

            add_loop(n, body, 2)

        def body(i, k):
            rv[pl.ds(l + i, k)] = total(i, k).astype(BF16)

        chunk = lambda d: self.shift(G.q, d) * G.Cq
        keep(0, chunk(0), G.Cq)
        keep(G.Cq, chunk(1), half)
        keep(G.Cq + half, chunk(-1) + half, half)
        add_loop(G.C, body, 8)

        def part(start, to, at, sem):
            self.send(rv.at[pl.ds(l + start, half)], rv.at[pl.ds(G.p2 + at, half)], self.s_rs.at[m, c], sem.at[m, c], G.q, to)

        part(chunk(2), 1, 0, self.s_qa)
        part(chunk(2) + half, -1, half, self.s_qa)
        part(chunk(1) + half, 1, G.Cq + half, self.s_p2)
        part(chunk(-1), -1, 2 * G.Cq, self.s_p2)

    def mid(self, m, c):
        G = geo(m, c)
        rv, half = self.recv.at[m, c], G.Cq // 2
        self.got(m, c, G.Cq, self.s_qa.at[m, c])

        def body(i, k):
            at = pl.ds(G.p2 + i, k)
            rv[at] = (self.own1[m % 2, c, pl.ds(G.Cq + i, k)] + rv[at].astype(F32)).astype(BF16)

        add_loop(G.Cq, body, 4)
        for at, dst, to in ((0, G.Cq, 1), (half, 2 * G.Cq + half, -1)):
            self.send(rv.at[pl.ds(G.p2 + at, half)], rv.at[pl.ds(G.p2 + dst, half)], self.s_rs.at[m, c], self.s_p2.at[m, c], G.q, to)

    def second(self, m, c):
        G = geo(m, c)
        rv = self.recv.at[m, c]
        left, right = G.p2 + G.Cq, G.p2 + 2 * G.Cq
        self.got(m, c, 2 * G.Cq, self.s_p2.at[m, c])

        def total(i, k):
            return self.own1[m % 2, c, pl.ds(i, k)] + rv[pl.ds(left + i, k)].astype(F32) + rv[pl.ds(right + i, k)].astype(F32)

        for k, d in enumerate((0, 2, -2) if G.long else (0,)):
            self.own2[m % RING, c, k] = total(self.shift(G.r, d) * SHARE, SHARE)

        def body(i, k):
            rv[pl.ds(left + i, k)] = total(i, k).astype(BF16)

        add_loop(G.Cq, body, 4)

        def piece(by, to, slot, sem):
            self.send(rv.at[pl.ds(left + self.shift(G.r, by) * SHARE, SHARE)], rv.at[pl.ds(G.p3 + SHARE * slot, SHARE)], self.s_rs.at[m, c], sem.at[m, c], G.r, to)

        if G.long:
            piece(3, 1, 0, self.s_za)
            piece(-3, -1, 1, self.s_za)
            piece(4, 2 * self.way, 2, self.s_za)
            piece(1, 1, 3, self.s_p3)
            piece(-1, -1, 4, self.s_p3)
        else:
            for d in range(1, G.nr):
                piece(d, d, d - 1, self.s_p3)

    def zmid(self, m, c):
        G = geo(m, c)
        rv = self.recv.at[m, c]
        self.got(m, c, 3 * SHARE, self.s_za.at[m, c])
        came = [rv[pl.ds(G.p3 + SHARE * i, SHARE)].astype(F32) for i in range(3)]
        ahead = self.own2[m % RING, c, 1] + came[0] + jnp.where(self.even, came[2], 0.0)
        behind = self.own2[m % RING, c, 2] + came[1] + jnp.where(self.even, 0.0, came[2])
        for slot, (way, piece) in enumerate(((2, ahead), (-2, behind))):
            rv[pl.ds(G.p3 + SHARE * slot, SHARE)] = piece.astype(BF16)
        for slot, way in enumerate((2, -2)):
            self.send(rv.at[pl.ds(G.p3 + SHARE * slot, SHARE)], rv.at[pl.ds(G.p3 + SHARE * (5 + slot), SHARE)], self.s_rs.at[m, c], self.s_p3.at[m, c], G.r, way)

    def third(self, m, c):
        G = geo(m, c)
        rv = self.recv.at[m, c]
        first, n = (3, 4) if G.long else (0, 3)
        self.got(m, c, SHARE * n, self.s_p3.at[m, c])
        t = self.own2[m % RING, c, 0]
        for i in range(first, first + n):
            t = t + rv[pl.ds(G.p3 + SHARE * i, SHARE)].astype(F32)
        t = t.astype(BF16)
        self.fin[m, c] = t
        t = t.astype(F32)
        return jnp.sum((t * t).reshape(6, 8, 128), axis=0)

    def rs_sent(self, m, c):
        G = geo(m, c)
        n = 4 * G.H + 2 * G.H + 2 * G.C * (G.h - 2) + (G.nq - 1) * G.Cq + (G.nr - 1) * 3
        self.wait(self.g.at[m], n, self.s_rs.at[m, c])

    def place(self, m, c, p, q=None, r=None):
        G = geo(m, c)
        return c * SLAB + p * G.C + (0 if q is None else q * G.Cq) + (0 if r is None else r * SHARE)

    def gather_r(self, m, c):
        G = geo(m, c)
        dst = self.out.at[m, pl.ds(self.place(m, c, self.at[G.p], self.at[G.q], self.at[G.r]), SHARE)]
        for d in (1, -1, 2, -2) if G.long else range(1, G.nr):
            self.send(self.fin.at[m, c], dst, self.s_ag.at[m, c], (self.s_zg if G.long else self.s_gr).at[m, c], G.r, d)
        pltpu.make_async_copy(self.fin.at[m, c], dst, self.s_loc.at[m, c]).start()

    def zpass(self, m, c):
        G = geo(m, c)
        self.wait(self.out.at[m], 4 * SHARE, self.s_zg.at[m, c])
        for by, to in ((-2, 1), (2, -1), (-2 * self.way, 2 * self.way)):
            ref = self.out.at[m, pl.ds(self.place(m, c, self.at[G.p], self.at[G.q], self.shift(G.r, by)), SHARE)]
            self.send(ref, ref, self.s_ag.at[m, c], self.s_gr.at[m, c], G.r, to)

    def gather_q(self, m, c):
        G = geo(m, c)
        self.wait(self.out.at[m], SHARE, self.s_loc.at[m, c])
        self.wait(self.out.at[m], 3 * SHARE, self.s_gr.at[m, c])
        ref = self.out.at[m, pl.ds(self.place(m, c, self.at[G.p], self.at[G.q]), G.Cq)]
        for d in (1, -1):
            self.send(ref, ref, self.s_ag.at[m, c], self.s_gq.at[m, c], G.q, d)

    def qpass(self, m, c):
        G = geo(m, c)
        self.wait(self.out.at[m], 2 * G.Cq, self.s_gq.at[m, c])
        half = G.Cq // 2
        for d, more in ((1, 0), (-1, half)):
            ref = self.out.at[m, pl.ds(self.place(m, c, self.at[G.p], self.shift(G.q, -d)) + more, half)]
            self.send(ref, ref, self.s_ag.at[m, c], self.s_gh.at[m, c], G.q, d)

    def gather_p(self, m, c, s):
        G = geo(m, c)
        if s == 1:
            self.wait(self.out.at[m], G.Cq, self.s_gh.at[m, c])
        else:
            self.wait(self.out.at[m], G.C, self.s_gl.at[m, c, s - 2])
            self.wait(self.out.at[m], G.C, self.s_gright.at[m, c, s - 2])
        n = G.C if s < G.h else G.H
        a = self.out.at[m, pl.ds(self.place(m, c, self.shift(G.p, 1 - s)), n)]
        b = self.out.at[m, pl.ds(self.place(m, c, self.shift(G.p, s - 1)) + (G.C - n), n)]
        self.send(a, a, self.s_ag.at[m, c], self.s_gl.at[m, c, s - 1], G.p, 1)
        self.send(b, b, self.s_ag.at[m, c], self.s_gright.at[m, c, s - 1], G.p, -1)

    def gathered(self, m, c):
        G = geo(m, c)
        self.wait(self.out.at[m], G.H, self.s_gl.at[m, c, G.h - 1])
        self.wait(self.out.at[m], G.H, self.s_gright.at[m, c, G.h - 1])
        n = 3 * (G.nr - 1) + (G.nq - 1) * G.Cq + 2 * G.C * (G.h - 1) + 2 * G.H
        self.wait(self.g.at[m], n, self.s_ag.at[m, c])


def comm_scratch(k):
    dma = pltpu.SemaphoreType.DMA
    one = dma((k, 3))
    return [
        pltpu.VMEM((k, 3, RECV) + TILE, BF16),
        pltpu.VMEM((RING, 3, OWN) + TILE, BF16),
        pltpu.VMEM((2, 3, 48) + TILE, F32),
        pltpu.VMEM((RING, 3, 3, SHARE) + TILE, F32),
        pltpu.VMEM((k, 3, 3) + TILE, BF16),
    ], [one] * 5 + [dma((k, 3, 3))] * 2 + [one] * 5 + [dma((k, 3, 4))] * 2 + [one] * 4


def norm_exchange(comm, acc, slots, s_send, s_recv):
    first, total = 0, acc[...]
    for i, ax in enumerate("xyz"):
        n = SIZE[ax]
        slots[pl.ds(first + comm.at[ax], 1)] = total[None]
        ref = slots.at[pl.ds(first + comm.at[ax], 1)]
        for d in range(1, n):
            comm.send(ref, ref, s_send.at[i], s_recv.at[i], ax, d)
        yield
        comm.wait(slots, n - 1, s_recv.at[i])
        total = slots[first]
        for k in range(1, n):
            total = total + slots[first + k]
        first += n
    yield total
    for i, ax in enumerate("xyz"):
        comm.wait(slots, SIZE[ax] - 1, s_send.at[i])


WIDE = 512
STEPS = FF // WIDE


LINK, PRODUCT, NEAR, FAR, HOP = 0.092, 2.6, 2.0, 3.1, 0.7
STORED, BRIEF, ADDS, ADD = 2.5, 0.05, 0.1, 0.002


def tasks(G):
    def each(ax, tiles, late, name):
        return [(ax, (tiles, 0), late, name), (ax, (0, tiles), late, name)]

    follow = lambda s: "first" if s == G.h else f"step{s + 1}"
    out = [("raw", (), each(G.p, G.H, FAR, "step2") + each(G.p, G.H, FAR, follow(2)), BRIEF)]
    for s in range(2, G.h + 1):
        n = G.H if s == 2 else G.C
        out.append((f"step{s}", (f"step{s}",), each(G.p, n, NEAR, follow(s)), ADDS + 4 * ADD * n))
    half = G.Cq / 2
    out.append(("first", ("first",), each(G.q, half, NEAR, "mid") + each(G.q, half, NEAR, "second"), ADDS + 3 * ADD * (G.C + G.Cq)))
    out.append(("mid", ("mid",), each(G.q, half, NEAR, "second"), ADDS + 2 * ADD * G.Cq))
    if G.long:
        far = each(G.r, SHARE, NEAR, "zmid") + [(G.r, (SHARE, SHARE), NEAR + HOP, "zmid")]
        out.append(("second", ("second",), far + each(G.r, SHARE, NEAR, "third"), ADDS + 4 * ADD * G.Cq))
        out.append(("zmid", ("zmid",), each(G.r, 2 * SHARE, NEAR + HOP, "third"), ADDS))
        out.append(("third", ("third",), [], ADDS + BRIEF))
        out.append(("gather1", (), each(G.r, SHARE, STORED, "zpass") + each(G.r, 2 * SHARE, STORED + HOP, "zpass"), BRIEF))
        out.append(("zpass", ("zpass",), each(G.r, SHARE, FAR, "gather2") + [(G.r, (SHARE, SHARE), FAR + HOP, "gather2")], BRIEF))
    else:
        out.append(("second", ("second",), each(G.r, SHARE, NEAR, "third") + [(G.r, (SHARE, SHARE), NEAR + HOP, "third")], ADDS + 4 * ADD * G.Cq))
        out.append(("third", ("third",), [], ADDS + BRIEF))
        out.append(("gather1", (), each(G.r, SHARE, STORED, "gather2") + [(G.r, (SHARE, SHARE), STORED + HOP, "gather2")], BRIEF))
    out.append(("gather2", ("gather2",), each(G.q, G.Cq, FAR, "qpass"), BRIEF))
    out.append(("qpass", ("qpass",), each(G.q, half, FAR, "along1"), BRIEF))
    for s in range(1, G.h + 1):
        out.append((f"along{s}", (f"along{s}",), each(G.p, G.C if s < G.h else G.H, FAR, f"along{s + 1}"), BRIEF))
    out.append(("end", (f"along{G.h + 1}",), [], BRIEF))
    return out


def schedule(k):
    lists = {(m, c): tasks(geo(m, c)) for m in range(k) for c in THREE}
    place = dict.fromkeys(lists, 0)
    arrived, free, done, order = {}, {}, set(), []
    now, steps = 3.0, 0
    while any(place[mc] < len(lists[mc]) for mc in lists):
        ready = []
        for (m, c), tasks_ in lists.items():
            if place[m, c] == len(tasks_):
                continue
            name, waits, _, _ = tasks_[place[m, c]]
            if name == "raw" and (steps < STEPS * m + (3 if c == 0 else STEPS) or m >= RING and (m - RING, c, "first") not in done):
                continue
            if name == "first" and (m >= RING and (m - RING, c, "third") not in done or m >= 2 and (m - 2, c, "second") not in done):
                continue
            when = max((arrived[m, c, w] for w in waits), default=0.0)
            ready.append((when, (name != "raw", m, c), m, c))
        here = [r for r in ready if r[0] <= now]
        if not here and steps < STEPS * k:
            now, steps = now + PRODUCT, steps + 1
            continue
        when, _, m, c = min(here, key=lambda r: r[1]) if here else min(ready)
        name, _, sends, takes = lists[m, c][place[m, c]]
        now = max(now, when) + takes
        for ax, tiles, late, to in sends:
            end = now
            for way in range(2):
                if tiles[way]:
                    end = free[ax, way] = max(free.get((ax, way), 0.0), now) + LINK * tiles[way]
            arrived[m, c, to] = max(arrived.get((m, c, to), 0.0), end + late)
        place[m, c] += 1
        done.add((m, c, name))
        order.append((steps, m, c, name))
    order = [e for e in order if e[3] != "end"]
    last = max(i for i, e in enumerate(order) if e[3] == "third")
    for i in range(4):
        after = min(last + 1 + NORM_GAP * i, len(order))
        order.insert(after, (order[after - 1][0], k, 0, f"norm{i}"))
    return order


NORM_GAP = 12


def gradients_kernel(k, pairs, *refs):
    lefts, rights = refs[:6], refs[6:12]
    g, out, ss_out, recv, own, own1, own2, fin, acc, slots, lbuf, rbuf, obuf, zero = refs[12:26]
    sems = refs[26:]
    comm = Comm(g, out, recv, own, own1, own2, fin, sems[:18])
    s_send, s_recv, s_left, s_right, s_out, s_zero = sems[18:]
    comm.barrier()
    acc[...] = jnp.zeros_like(acc)
    zero[...] = jnp.zeros_like(zero)

    def left(m):
        return pltpu.make_async_copy(lefts[m], lbuf.at[m % 2], s_left.at[m % 2])

    def right(m, j):
        slot = (m * STEPS + j) % 2
        return pltpu.make_async_copy(rights[m].at[:, pl.ds(j * WIDE, WIDE)], rbuf.at[slot], s_right.at[slot])

    def put(m, j):
        slot = (m * STEPS + j) % 2
        return pltpu.make_async_copy(obuf.at[slot], g.at[m, pl.ds(j * 4 * BANDS, 4 * BANDS)], s_out.at[slot])

    def blank(m):
        return pltpu.make_async_copy(zero, g.at[m, pl.ds(1120, 32)], s_zero.at[m])

    left(0).start()
    right(0, 0).start()
    for m in range(k):
        blank(m).start()
    for m in range(k):
        blank(m).wait()

    norm = norm_exchange(comm, acc, slots, s_send, s_recv)

    def run(m, c, name):
        if name.startswith("norm"):
            total = next(norm)
            if name == "norm3":
                ss_out[...] = total
                for _ in norm:
                    pass
        elif name == "raw":
            comm.raw(m, c)
            comm.load(m, c)
        elif name.startswith("step"):
            comm.step(m, c, int(name[4:]))
        elif name == "third":
            acc[...] += comm.third(m, c)
        elif name == "gather1":
            comm.gather_r(m, c)
        elif name == "gather2":
            comm.gather_q(m, c)
        elif name.startswith("along"):
            comm.gather_p(m, c, int(name[5:]))
        else:
            getattr(comm, name)(m, c)

    events = schedule(k)
    for m in range(k):
        left(m).wait()

        @pl.loop(0, STEPS)
        def _(j):
            right(m, j).wait()

            @pl.when(j < STEPS - 1)
            def _():
                right(m, j + 1).start()

            if m + 1 < k:
                @pl.when(j == STEPS - 1)
                def _():
                    right(m + 1, 0).start()

                @pl.when(j == 1)
                def _():
                    left(m + 1).start()

            slot = (m * STEPS + j) % 2
            v = dot(lbuf[m % 2], rbuf[slot], TN).astype(BF16)
            for c in range(WIDE // LANES):
                obuf[slot, c * BANDS:(c + 1) * BANDS] = v[:, c * LANES:(c + 1) * LANES].reshape((BANDS,) + TILE)
            put(m, j).start()

            @pl.when(j >= 1)
            def _():
                put(m, j - 1).wait()

            for n in range(STEPS - 1):
                now = [e[1:] for e in events if e[0] == STEPS * m + n + 1]
                if now:
                    @pl.when(j == n)
                    def _():
                        for e in now:
                            run(*e)

        put(m, STEPS - 1).wait()
        for e in events:
            if e[0] == STEPS * (m + 1):
                run(*e[1:])
    for m in range(k):
        for c in THREE:
            comm.rs_sent(m, c)
            comm.gathered(m, c)


def gradients(x, dy, w_gate, w_up, w_down):
    a0, z0, dg0, du0, a1, z1, dg1, du1, dh = activations(x, dy, w_gate, w_up, w_down, CH=256)
    return (dy, a1, a1, dh, a0, a0), (z1, dg1, du1, z0, dg0, du0)


def summed(lefts, rights):
    k = 6
    bufs, sems = comm_scratch(k)
    dma = pltpu.SemaphoreType.DMA
    return pl.pallas_call(
        functools.partial(gradients_kernel, k, tuple(range(6))),
        name="gradients",
        out_shape=(jax.ShapeDtypeStruct((k, NT) + TILE, BF16), jax.ShapeDtypeStruct((k, NT) + TILE, BF16), jax.ShapeDtypeStruct(SQUARES, F32)),
        in_specs=[ANY] * 12,
        out_specs=(ANY, ANY, pl.BlockSpec(memory_space=pltpu.VMEM)),
        scratch_shapes=bufs + [pltpu.VMEM(SQUARES, F32), pltpu.VMEM((16,) + SQUARES, F32),
                               pltpu.VMEM((2, S, D), BF16), pltpu.VMEM((2, S, 512), BF16), pltpu.VMEM((2, 224) + TILE, BF16), pltpu.VMEM((32,) + TILE, BF16)]
        + sems + [dma((3,))] * 2 + [dma((2,))] * 3 + [dma((k,))],
        cost_estimate=pl.CostEstimate(flops=12 * S * D * FF, bytes_accessed=12 * S * (D + FF), transcendentals=0),
        compiler_params=pltpu.CompilerParams(collective_id=0, has_side_effects=True, vmem_limit_bytes=MOST),
    )(*lefts, *rights)


def solution(mesh):
    def step(x, dy, w_gate, w_up, w_down, m_gate, m_up, m_down, v_gate, v_up, v_down):
        _, g, ss = summed(*gradients(x[0], dy[0], w_gate, w_up, w_down))
        return tuple(adamw(ss, g, (w_gate, w_up, w_down), (m_gate, m_up, m_down), (v_gate, v_up, v_down)))

    return jax.shard_map(
        step,
        mesh=mesh,
        in_specs=(P(("rep", "dp")),) * 2 + (P(),) * 9,
        out_specs=(P("rep"),) * 9,
        check_vma=False,
    )
```

time: 505 us -> 464 us (0.919)
  Pallas kernels: 503 us -> 462 us
    pallas_call x1, Pallas kernels: 275 us -> 247 us  [summed(): pl.pallas_call(functools.partial(gradients_kernel, k, tuple(range(6))), n...]
    pallas_call x3 -> x1, Pallas kernels: 110 us -> 96.9 us  [adamw(): pl.pallas_call(functools.partial(adamw_kernel, B), name='adamw', in_specs...]
where the time goes in v2:
time: 464 us; the launch traced here: 462 us
  Pallas kernels  462 us (100%)
    pallas_call x1, Pallas kernels, summed(): pl.pallas_call(functools.partial(gradients_kernel, k, tuple(range(6))), n...  247 us
    pallas_call x1, Pallas kernels, activations(): pl.pallas_call(functools.partial(activations_kernel, CH), name='activatio...  118 us
    pallas_call x1, Pallas kernels, adamw(): pl.pallas_call(functools.partial(adamw_kernel, B), name='adamw', in_specs...  96.9 us

profile of v2, /device:TPU:2, one launch (start us, length us, event | category | flops | bytes accessed | tf_op | source)
XLA Modules:
  0.0 462.5 jit_solution(7461462926156724569)
XLA Ops:
  0.6 117.5 %activations.1 = (bf16[2048,896]{1,0:T(8,128)(2,1)}, bf16[2048,2560]{1,0:T(8,128)(2,1)}, bf16[2048,2560]{1,0:T(8,128)(2,1)}, bf16[2048,2560]{1,0:T(8,128)(2,1)},...) custom-call(bf16[2048,896]{1,0:T(8,128)(2,1)} %bitcast.2, ...), custom_call_target="tpu_custom_call" | custom-call | flops 84557168640 | bytes 108789760 | tf_op jit(solution)/shard_map/activations/pallas_call | solution.py:107
  118.2 247.2 %gradients.1 = (bf16[6,1152,16,128]{3,2,1,0:T(8,128)(2,1)}, bf16[6,1152,16,128]{3,2,1,0:T(8,128)(2,1)}, f32[8,128]{1,0:T(8,128)}) custom-call(bf16[2048,896]{1,0:T(8,128)(2,1)} %bitcast.4, bf16[2048,896]{1,0:T(8,128)(2,1)} %get-tuple-element.20.refs_1_.refs_2_, bf16[2048,896]{1,0:T(8,128)(2,1)} %get-tuple-element.20.refs_1_.refs_2_, ...), custom_call_target="tpu_custom_call" | custom-call | flops 56371445760 | bytes 84934656 | tf_op jit(solution)/shard_map/gradients/pallas_call | solution.py:738
  365.4 96.9 %adamw.1 = (bf16[2,896,2560]{2,1,0:T(8,128)(2,1)}, bf16[2,896,2560]{2,1,0:T(8,128)(2,1)}, bf16[2,2560,896]{2,1,0:T(8,128)(2,1)}, f32[2,896,2560]{2,1,0:T(8,128)}...) custom-call(f32[8,128]{1,0:T(8,128)} %get-tuple-element.29.ss_ref, ...), custom_call_target="tpu_custom_call" | custom-call | flops 275251200 | bytes 302776320 | tf_op jit(solution)/shard_map/adamw/pallas_call | solution.py:201
